TPU v7x, 32 devices: a 4x4x1 block of a 4x4x8 slice. The times are simulated.
32 devices in a mesh: dp: 2 (over z, core), tp: 16 (over x, y).
Axes of the slice: x: 4, y: 4, z: 1, core: 2. Of those that a mesh axis runs over, the one named last changes fastest.
The devices are a block of a 4x4x8 slice.
Arguments:
- x: bfloat16 [128, 3072], P('dp'), parts along dimension 0
- k_cache: bfloat16 [128, 2048, 16, 256], P('dp', None, 'tp'), parts along dimension 0
- v_cache: bfloat16 [128, 2048, 16, 256], P('dp', None, 'tp'), parts along dimension 0
- gain_a: bfloat16 [3072], replicated
- wq: bfloat16 [3072, 4096], P(None, 'tp')
- wo: bfloat16 [4096, 3072], P('tp')
- gain_m: bfloat16 [3072], replicated
- w_gate: bfloat16 [3072, 24576], P(None, 'tp')
- w_up: bfloat16 [3072, 24576], P(None, 'tp')
- w_down: bfloat16 [24576, 3072], P('tp')
Outputs:
- output: bfloat16 [128, 3072], P('dp'), parts along dimension 0
There are 2 independent parts. A program takes and returns all parts, laid end to end along the dimension named above; an argument that names none is the same for every part.
All inputs are finite; a program needn't handle non-finite values.
Results may differ from a plain program's by a relative error of at most 0.017.
Values are sent between devices in bfloat16 or wider.
A program may use at most 768 MiB of HBM per device.

v0:
```python
import jax
import jax.numpy as jnp
from jax import lax
from jax.sharding import PartitionSpec as P

HEAD = 256
THETA = 10000


def normed(x, gain):
    wide = x.astype(jnp.float32)
    scale = lax.rsqrt(jnp.mean(wide * wide, -1, keepdims=True) + 1e-6)
    return (wide * scale * gain.astype(jnp.float32)).astype(jnp.bfloat16)


def turned(t, place, theta):
    half = t.shape[-1] // 2
    angle = place.astype(jnp.float32)[:, None] * theta ** (-jnp.arange(half, dtype=jnp.float32) / half)
    cos, sin = jnp.cos(angle)[:, None], jnp.sin(angle)[:, None]
    a, b = t[..., :half].astype(jnp.float32), t[..., half:].astype(jnp.float32)
    return jnp.concatenate([a * cos - b * sin, b * cos + a * sin], -1).astype(jnp.bfloat16)


def matmul(a, w):
    return jnp.dot(a, w, preferred_element_type=jnp.float32).astype(jnp.bfloat16)


def einsum(form, a, b):
    return jnp.einsum(form, a.astype(jnp.float32), b.astype(jnp.float32))


def seen_by(a, wq, k_cache, v_cache, head, theta):
    batch, cache, kv_heads = k_cache.shape[:3]
    place = jnp.full((batch,), cache - 1)
    q = turned(matmul(a, wq).reshape(batch, -1, head), place, theta).reshape(batch, kv_heads, -1, head)
    scores = einsum("bgsd,bugd->bgsu", q, k_cache) * head**-0.5
    weights = jax.nn.softmax(scores, -1).astype(jnp.bfloat16)
    return einsum("bgsu,bugd->bgsd", weights, v_cache).astype(jnp.bfloat16).reshape(batch, -1)


def hidden_of(b, w_gate, w_up):
    gate = jnp.dot(b, w_gate, preferred_element_type=jnp.float32)
    up = jnp.dot(b, w_up, preferred_element_type=jnp.float32)
    return (jax.nn.silu(gate) * up).astype(jnp.bfloat16)


def solution(mesh):
    def added(t, term):
        return (t.astype(jnp.float32) + lax.psum(term.astype(jnp.bfloat16), "tp").astype(jnp.float32)).astype(jnp.bfloat16)

    def step(x, k_cache, v_cache, gain_a, wq, wo, gain_m, w_gate, w_up, w_down):
        seen = seen_by(normed(x, gain_a), wq, k_cache, v_cache, HEAD, THETA)
        h = added(x, jnp.dot(seen, wo, preferred_element_type=jnp.float32))
        return added(h, jnp.dot(hidden_of(normed(h, gain_m), w_gate, w_up), w_down, preferred_element_type=jnp.float32))

    states, cache, columns, rows_of = P("dp", None), P("dp", None, "tp", None), P(None, "tp"), P("tp", None)
    return jax.shard_map(
        step,
        mesh=mesh,
        in_specs=(states, cache, cache, P(None), columns, rows_of, P(None), columns, columns, rows_of),
        out_specs=states,
        check_vma=False,
    )
```

profile of v0, /device:TPU:96, one launch (start us, length us, event | category | flops | bytes accessed | tf_op | source)
XLA Modules:
  0.0 238.5 jit_solution(1970265862499182134)
XLA Ops:
  6.5 0.0 copy-start
  6.6 0.0 all-reduce.3.cloned.1.call-start
  6.6 1.3 fusion.6
  7.9 0.7 convert_element_type.68
  8.6 2.0 fusion.5
  10.6 25.4 %fusion.2 = f32[64,1,2048]{2,1,0:T(1,128)S(1)} fusion(bf16[64,2048,1,256]{3,1,2,0:T(8,128)(2,1)} %param.11, bf16[64,256,1]{1,0,2:T(8,128)(2,1)S(1)} %maximum_bitcast_fusion), kind=kOutput, calls=%fused_computation.2 | convolution fusion | flops 67108864 | bytes 67665920 | tf_op jit(solution)/shard_map/bgsd,bugd->bgsu/dot_general | solution.py:29
  36.0 0.3 fusion.16
  36.3 0.3 fusion.15
  36.6 0.2 fusion.25
  36.8 0.0 copy-start.2
  36.8 0.0 copy-start.1
  36.8 22.7 %fusion = bf16[64,1,256]{2,1,0:T(2,128)(2,1)S(1)} fusion(bf16[64,2048,1,256]{3,1,2,0:T(8,128)(2,1)} %param.12, bf16[64,2048,1]{1,0,2:T(8,128)(2,1)S(1)} %fusion.25), kind=kOutput, calls=%fused_computation | convolution fusion | flops 67108864 | bytes 67403776 | tf_op jit(solution)/shard_map/bgsu,bugd->bgsd/dot_general | solution.py:29
  59.6 0.0 copy-done
  59.6 1.1 convolution_convert_fusion.1
  60.7 0.1 all-reduce.3.cloned.1.call-update
  60.8 0.1 all-reduce.5.cloned.1.call-start
  60.8 0.0 copy-done.2
  60.9 77.3 %all-reduce.3.cloned.1.call-done = bf16[64,3072]{1,0:T(8,128)(2,1)} async-done(((bf16[64,3072]{1,0:T(8,128)(2,1)}), bf16[64,3072]{1,0:T(8,128)(2,1)}) %all-reduce.3.cloned.1.call-update) | async-done | bytes 393232 | tf_op jit(solution)/shard_map/psum | solution.py:49
  138.2 0.0 copy-done.1
  138.2 1.2 fusion.10
  139.4 5.5 %fusion.29 = f32[64,1536]{1,0:T(8,128)S(1)} fusion(bf16[3072,1536]{1,0:T(8,128)(2,1)} %param.17, bf16[64,3072]{1,0:T(8,128)(2,1)S(1)} %get-tuple-element.6, f32[3072]{0:T(1024)S(1)} %convert_element_type.79, f32[64]{0:T(128)S(1)} %add_rsqrt_fusion), kind=kOutput, calls=%fused_computation.39 | convolution fusion | flops 604766208 | bytes 10236160 | tf_op jit(solution)/shard_map/dot_general | solution.py:42
  144.9 10.6 %convolution_convert_fusion = bf16[64,3072]{1,0:T(8,128)(2,1)} fusion(bf16[1536,3072]{1,0:T(8,128)(2,1)} %param.19, bf16[3072,1536]{1,0:T(8,128)(2,1)} %param.18, f32[64,1536]{1,0:T(8,128)S(1)} %fusion.29, bf16[64,3072]{1,0:T(8,128)(2,1)S(1)} %get-tuple-element.6, f32[3072]{0:T(1024)S(1)} %convert_element_type.79, f32[64]{0:T(128)S(1)} %add_rsqrt_fusion), kind=kOutput, calls=%fused_computation.4 | convolution fusion | flops 1209532416 | bytes 20066560 | tf_op jit(solution)/shard_map/dot_general | solution.py:54
  155.5 0.1 all-reduce.5.cloned.1.call-update
  155.6 74.2 %all-reduce.5.cloned.1.call-done = bf16[64,3072]{1,0:T(8,128)(2,1)} async-done(((bf16[64,3072]{1,0:T(8,128)(2,1)}), bf16[64,3072]{1,0:T(8,128)(2,1)}) %all-reduce.5.cloned.1.call-update) | async-done | bytes 393232 | tf_op jit(solution)/shard_map/psum | solution.py:49
  229.8 1.8 fusion.13
  (6 shorter events, 0.1 us)
Async XLA Ops:
  6.5 53.0 %copy-start = (bf16[256,3072]{1,0:T(8,128)(2,1)S(1)}, bf16[256,3072]{1,0:T(8,128)(2,1)}, u32[]{:S(2)}) copy-start(bf16[256,3072]{1,0:T(8,128)(2,1)} %param.15) | copy-start | bytes 4718596
  6.6 131.6 %all-reduce.3.cloned.1.call-start = ((), (), s32[]{:S(2)}) async-start(), calls=%async_computation | async-start | bytes 786432 | tf_op jit(solution)/shard_map/psum | solution.py:49
  36.8 24.1 %copy-start.2 = (bf16[3072]{0:T(1024)(128)(2,1)S(1)}, bf16[3072]{0:T(1024)(128)(2,1)}, u32[]{:S(2)}) copy-start(bf16[3072]{0:T(1024)(128)(2,1)} %param.16) | copy-start | bytes 18436
  36.8 101.4 %copy-start.1 = (bf16[64,3072]{1,0:T(8,128)(2,1)S(1)}, bf16[64,3072]{1,0:T(8,128)(2,1)}, u32[]{:S(2)}) copy-start(bf16[64,3072]{1,0:T(8,128)(2,1)} %param.10) | copy-start | bytes 1179652
  60.8 169.0 %all-reduce.5.cloned.1.call-start = ((), (), s32[]{:S(2)}) async-start(), calls=%async_computation.1 | async-start | bytes 786432 | tf_op jit(solution)/shard_map/psum | solution.py:49
Sparse Core Ops, SparseCore 0:
  60.9 77.2 all-reduce.2
  155.7 74.0 all-reduce.4
where the time goes:
time: 239 us; the launch traced here: 238 us
  waiting for transfers between devices  152 us (64%)
  matrix products  67.3 us (28%)
  between operations  13.5 us (6%)
  other arithmetic  5.96 us (2%)
    psum x2, waiting for transfers between devices, added(): lax.psum(term.astype(jnp.bfloat16), 'tp').astype(jnp.float32)  152 us
    dot_general x2, matrix products, einsum(): return jnp.einsum(form, a.astype(jnp.float32), b.astype(jnp.float32))  48.1 us
    dot_general x1, matrix products, step(): jnp.dot(hidden_of(normed(h, gain_m), w_gate, w_up), w_down, preferred_ele...  10.6 us
    dot_general x1, matrix products, hidden_of(): gate = jnp.dot(b, w_gate, preferred_element_type=jnp.float32)  5.49 us
  transfers between devices with their start and end apart: 2, of which 2 were waited for; matrix products, arithmetic and copies ran while one was open for 0% of the time, Pallas kernels for 0%

commit v1 on v0

v1 whole, which is shorter than its diff:
```python
import functools

import jax
import jax.numpy as jnp
import numpy as np
from jax import lax
from jax.experimental import pallas as pl
from jax.experimental.pallas import tpu as pltpu
from jax.sharding import PartitionSpec as P

THETA = 10000
EPS = 1e-6
GROUP = 8
PIECE = 4
CHUNK = 16
SUB = 8
MESH = pl.DeviceIdType.MESH
BF16, F32 = jnp.bfloat16, jnp.float32


def normed(wide, gain):
    scale = lax.rsqrt(jnp.mean(wide * wide, -1, keepdims=True) + EPS)
    return (wide * scale * gain).astype(BF16)


def dot(a, b):
    return jnp.dot(a, b, preferred_element_type=F32)


def kernel(n, x_hbm, k_hbm, v_hbm, ga_hbm, wq_hbm, wo_hbm, gm_hbm, wg_hbm, wu_hbm, wd_hbm, trig_hbm, out_ref,
           x_v, ga_v, gm_v, trig_v, wq_v, wo_v, wg_v, wu_v, wd_v, ring, x32, h32, q32, seen32, act, hidden,
           own1, term1, rs1, hb, own2, term2, rs2, yb,
           in_sem, w_sem, ring_sem, send1, recv1, send2, recv2, send3, recv3, send4, recv4):
    me = lax.axis_index("tp")
    rows, d = x_v.shape
    head = q32.shape[1]
    half = head // 2
    groups = rows // GROUP
    chunks = rows // CHUNK
    cols1 = d * CHUNK // (n * SUB)
    per_row1 = d // cols1
    width2 = d // chunks
    per_row2 = width2 // cols1

    def fetch(src, dst, sem):
        return pltpu.make_async_copy(src, dst, sem)

    small = [
        fetch(x_hbm, x_v, in_sem.at[0]),
        fetch(ga_hbm, ga_v, in_sem.at[1]),
        fetch(wq_hbm, wq_v, in_sem.at[2]),
        fetch(trig_hbm, trig_v, in_sem.at[3]),
        fetch(wo_hbm, wo_v, in_sem.at[4]),
        fetch(gm_hbm, gm_v, in_sem.at[5]),
    ]
    weights = [fetch(wg_hbm, wg_v, w_sem.at[0]), fetch(wu_hbm, wu_v, w_sem.at[1]), fetch(wd_hbm, wd_v, w_sem.at[2])]

    def piece(g, j):
        src = k_hbm if j < 2 else v_hbm
        return fetch(src.at[pl.ds(g * GROUP + (j % 2) * PIECE, PIECE)], ring.at[j], ring_sem.at[j])

    for c in small[:4]:
        c.start()
    for j in range(4):
        piece(0, j).start()
    for c in small[4:]:
        c.start()

    barrier = pltpu.get_barrier_semaphore()
    for r in range(1, n):
        pl.semaphore_signal(barrier, inc=1, device_id={"tp": lax.rem(me + r, n)}, device_id_type=MESH)

    small[0].wait()
    small[1].wait()
    wide = x_v[...].astype(F32)
    x32[...] = wide
    act[...] = normed(wide, ga_v[...].astype(F32))
    small[2].wait()
    small[3].wait()
    q = dot(act[...], wq_v[...]).astype(BF16).astype(F32)
    cos, sin = trig_v[0:1, :], trig_v[1:2, :]
    a, b = q[:, :half], q[:, half:]
    q32[:, :half] = (a * cos - b * sin).astype(BF16).astype(F32)
    q32[:, half:] = (b * cos + a * sin).astype(BF16).astype(F32)
    small[4].wait()
    small[5].wait()
    pl.semaphore_wait(barrier, n - 1)

    def total(buf, sem):
        fetch(buf.at[pl.ds(0, n - 1)], buf.at[pl.ds(0, n - 1)], sem).wait()

    def scatter(term, land, send, recv):
        for r in range(1, n):
            to = lax.rem(me + r, n)
            pltpu.make_async_remote_copy(
                src_ref=term.at[to], dst_ref=land.at[r - 1], send_sem=send, recv_sem=recv, device_id={"tp": to}, device_id_type=MESH
            ).start()

    def gather(buf, send, recv):
        for r in range(1, n):
            to = lax.rem(me + r, n)
            pltpu.make_async_remote_copy(
                src_ref=buf.at[me], dst_ref=buf.at[me], send_sem=send, recv_sem=recv, device_id={"tp": to}, device_id_type=MESH
            ).start()

    def summed(own, land):
        s = own[me]
        for r in range(n - 1):
            s = s + land[r].astype(F32)
        return s

    def send_first(c):
        res = dot(seen32[pl.ds(pl.multiple_of(c * CHUNK, CHUNK), CHUNK), :].astype(BF16), wo_v[...])
        for s in range(n):
            rg, cg = divmod(s, per_row1)
            part = res[rg * SUB : (rg + 1) * SUB, cg * cols1 : (cg + 1) * cols1]
            own1[s] = part
            term1[c, s] = part.astype(BF16)
        scatter(term1.at[c], rs1.at[c], send1.at[c], recv1.at[c])

    def sum_first(c):
        total(rs1.at[c], recv1.at[c])
        s = summed(own1, rs1.at[c])
        row = pl.multiple_of(c * CHUNK + me // per_row1 * SUB, SUB)
        col = pl.multiple_of(lax.rem(me, per_row1) * cols1, 128)
        hb[c, me] = (x32[pl.ds(row, SUB), pl.ds(col, cols1)] + s).astype(BF16)
        gather(hb.at[c], send2.at[c], recv2.at[c])

    row_of = lax.broadcasted_iota(jnp.int32, (GROUP, 1), 0)

    def group(g, carry):
        def refill(j):
            @pl.when(g < groups - 1)
            def _():
                piece(g + 1, j).start()

            if j < 3:
                @pl.when(g == groups - 1)
                def _():
                    weights[j].start()

        qg = q32[pl.ds(pl.multiple_of(g * GROUP, GROUP), GROUP), :]
        s = None
        for j in range(2):
            piece(g, j).wait()
            for i in range(PIECE):
                qm = jnp.where(row_of == j * PIECE + i, qg, 0.0).astype(BF16)
                t = lax.dot_general(qm, ring[j, i], (((1,), (1,)), ((), ())), preferred_element_type=F32)
                s = t if s is None else s + t
            refill(j)
        s = s * head**-0.5
        p = jnp.exp(s - jnp.max(s, -1, keepdims=True))
        w = p / jnp.sum(p, -1, keepdims=True)
        o = None
        for j in range(2, 4):
            piece(g, j).wait()
            for i in range(PIECE):
                wm = jnp.where(row_of == (j - 2) * PIECE + i, w, 0.0).astype(BF16)
                t = dot(wm, ring[j, i])
                o = t if o is None else o + t
            refill(j)
        seen32[pl.ds(pl.multiple_of(g * GROUP, GROUP), GROUP), :] = o
        per = CHUNK // GROUP

        @pl.when(lax.rem(g, per) == per - 1)
        def _():
            send_first(g // per)

        @pl.when(jnp.logical_and(lax.rem(g, per) == 0, g > 0))
        def _():
            sum_first(g // per - 1)

        return carry

    lax.fori_loop(0, groups, group, 0)
    sum_first(chunks - 1)

    gm = gm_v[...].astype(F32)
    for c in range(chunks):
        total(hb.at[c], recv2.at[c])
        h = jnp.concatenate(
            [
                jnp.concatenate([hb[c, rg * per_row1 + cg].astype(F32) for cg in range(per_row1)], 1)
                for rg in range(CHUNK // SUB)
            ],
            0,
        )
        h32[c * CHUNK : (c + 1) * CHUNK, :] = h
        act[c * CHUNK : (c + 1) * CHUNK, :] = normed(h, gm)

    weights[0].wait()
    weights[1].wait()
    block = 256

    def up(i, carry):
        at = pl.ds(pl.multiple_of(i * block, block), block)
        gate = dot(act[...], wg_v[:, at])
        hidden[:, at] = (jax.nn.silu(gate) * dot(act[...], wu_v[:, at])).astype(BF16)
        return carry

    lax.fori_loop(0, wg_v.shape[1] // block, up, 0)
    weights[2].wait()

    for c in range(chunks):
        res = dot(hidden[...], wd_v[:, c * width2 : (c + 1) * width2])
        for s in range(n):
            rg, cg = divmod(s, per_row2)
            part = res[rg * SUB : (rg + 1) * SUB, cg * cols1 : (cg + 1) * cols1]
            own2[c, s] = part
            term2[c, s] = part.astype(BF16)
        scatter(term2.at[c], rs2.at[c], send3.at[c], recv3.at[c])

    for c in range(chunks):
        total(rs2.at[c], recv3.at[c])
        s = summed(own2.at[c], rs2.at[c])
        row = pl.multiple_of(me // per_row2 * SUB, SUB)
        col = pl.multiple_of(c * width2 + lax.rem(me, per_row2) * cols1, 128)
        yb[c, me] = (h32[pl.ds(row, SUB), pl.ds(col, cols1)] + s).astype(BF16)
        gather(yb.at[c], send4.at[c], recv4.at[c])

    for c in range(chunks):
        total(yb.at[c], recv4.at[c])
        for rg in range(0, rows // SUB, 2):
            for cg in range(per_row2):
                pair = [yb[c, (rg + k) * per_row2 + cg].astype(F32) for k in range(2)]
                col = c * width2 + cg * cols1
                out_ref[rg * SUB : (rg + 2) * SUB, col : col + cols1] = jnp.concatenate(pair, 0).astype(BF16)

    for c in range(chunks):
        total(term1.at[c], send1.at[c])
        total(hb.at[c], send2.at[c])
        total(term2.at[c], send3.at[c])
        total(yb.at[c], send4.at[c])


def solution(mesh):
    n = mesh.shape["tp"]

    def step(x, k_cache, v_cache, gain_a, wq, wo, gain_m, w_gate, w_up, w_down):
        rows, d = x.shape
        cache = k_cache.shape[1]
        head = k_cache.shape[3]
        ff = w_gate.shape[1]
        half = head // 2
        angle = (cache - 1) * float(THETA) ** (-np.arange(half, dtype=np.float64) / half)
        trig = jnp.asarray(np.stack([np.cos(angle), np.sin(angle)]).astype(np.float32))
        chunks = rows // CHUNK
        share = (SUB, rows * d // chunks // n // SUB)
        any_spec = pl.BlockSpec(memory_space=pl.ANY)
        dma = pltpu.SemaphoreType.DMA
        call = pl.pallas_call(
            functools.partial(kernel, n),
            out_shape=jax.ShapeDtypeStruct((rows, d), BF16),
            in_specs=[any_spec] * 11,
            out_specs=pl.BlockSpec(memory_space=pltpu.VMEM),
            scratch_shapes=[
                pltpu.VMEM((rows, d), BF16),
                pltpu.VMEM((1, d), BF16),
                pltpu.VMEM((1, d), BF16),
                pltpu.VMEM((2, half), F32),
                pltpu.VMEM((d, head), BF16),
                pltpu.VMEM((head, d), BF16),
                pltpu.VMEM((d, ff), BF16),
                pltpu.VMEM((d, ff), BF16),
                pltpu.VMEM((ff, d), BF16),
                pltpu.VMEM((4, PIECE, cache, head), BF16),
                pltpu.VMEM((rows, d), F32),
                pltpu.VMEM((rows, d), F32),
                pltpu.VMEM((rows, head), F32),
                pltpu.VMEM((rows, head), F32),
                pltpu.VMEM((rows, d), BF16),
                pltpu.VMEM((rows, ff), BF16),
                pltpu.VMEM((n, *share), F32),
                pltpu.VMEM((chunks, n, *share), BF16),
                pltpu.VMEM((chunks, n - 1, *share), BF16),
                pltpu.VMEM((chunks, n, *share), BF16),
                pltpu.VMEM((chunks, n, *share), F32),
                pltpu.VMEM((chunks, n, *share), BF16),
                pltpu.VMEM((chunks, n - 1, *share), BF16),
                pltpu.VMEM((chunks, n, *share), BF16),
                dma((6,)),
                dma((3,)),
                dma((4,)),
            ]
            + [dma((chunks,))] * 8,
            compiler_params=pltpu.CompilerParams(collective_id=0, has_side_effects=True, vmem_limit_bytes=63 * 2**20),
        )
        flat = (rows, cache, head)
        return call(
            x, k_cache.reshape(flat), v_cache.reshape(flat), gain_a.reshape(1, d), wq, wo, gain_m.reshape(1, d), w_gate, w_up, w_down, trig
        )

    states, cache, columns, rows_of = P("dp", None), P("dp", None, "tp", None), P(None, "tp"), P("tp", None)
    return jax.shard_map(
        step,
        mesh=mesh,
        in_specs=(states, cache, cache, P(None), columns, rows_of, P(None), columns, columns, rows_of),
        out_specs=states,
        check_vma=False,
    )
```

time: 239 us -> 93.2 us (0.39)
  waiting for transfers between devices: 152 us -> 0 us
  Pallas kernels: 0 us -> 88.7 us
  matrix products: 67.3 us -> 0 us
  between operations: 13.5 us -> 0.01 us
  other arithmetic: 5.96 us -> 0 us
  local copies, waits for them, and re-layouts: 0.02 us -> 4.36 us
    psum x2 -> x0, waiting for transfers between devices: 152 us -> none  [added(): lax.psum(term.astype(jnp.bfloat16), 'tp').astype(jnp.float32)]
    pallas_call x0 -> x1, Pallas kernels: none -> 88.7 us  [step(): call(x, k_cache.reshape(flat), v_cache.reshape(flat), gain_a.reshape(1, d...]
    dot_general x6 -> x0, matrix products: 67.3 us -> none  [the longest x2 48.1 us: einsum(): return jnp.einsum(form, a.astype(jnp.float32), b.astype(jnp.float32))]
    reduce_sum x3 -> x0, other arithmetic: 2.83 us -> none  [the longest x2 2.52 us: normed(): scale = lax.rsqrt(jnp.mean(wide * wide, -1, keepdims=True) + 1e-06)]
    convert_element_type x4 -> x0, other arithmetic: 2.76 us -> none  [the longest x1 1.83 us: added(): (t.astype(jnp.float32) + lax.psum(term.astype(jnp.bfloat16), 'tp').astype...]
    reshape x0 -> x2, local copies, waits for them, and re-layouts: none -> 2.59 us  [the longest x1 1.3 us: step(): gain_a.reshape(1, d)]
  transfers between devices with their start and end apart: 2 -> 0, of which waited for: 2 -> 0; matrix products, arithmetic and copies ran while one was open for 0% -> 0% of each run, Pallas kernels for 0% -> 0%
where the time goes in v1:
time: 93.2 us; the launch traced here: 93 us
  Pallas kernels  88.7 us (95%)
  local copies, waits for them, and re-layouts  4.36 us (5%)
    pallas_call x1, Pallas kernels, step(): call(x, k_cache.reshape(flat), v_cache.reshape(flat), gain_a.reshape(1, d...  88.7 us

profile of v1, /device:TPU:96, one launch (start us, length us, event | category | flops | bytes accessed | tf_op | source)
XLA Modules:
  0.0 93.0 jit_solution(14880223367472830500)
XLA Ops:
  0.0 1.3 %reshape.14.ga_hbm = bf16[1,3072]{1,0:T(2,128)(2,1)} reshape(bf16[3072]{0:T(1024)(128)(2,1)} %param.14) | data formatting | bytes 12288 | tf_op jit(solution)/shard_map/reshape | solution.py:290
  1.3 1.3 %reshape.15.gm_hbm = bf16[1,3072]{1,0:T(2,128)(2,1)} reshape(bf16[3072]{0:T(1024)(128)(2,1)} %param.17) | data formatting | bytes 12288 | tf_op jit(solution)/shard_map/reshape | solution.py:290
  2.6 88.7 %shard_map.109 = bf16[64,3072]{1,0:T(8,128)(2,1)} custom-call(bf16[64,3072]{1,0:T(8,128)(2,1)} %x_hbm.1, bf16[64,2048,256]{2,1,0:T(8,128)(2,1)} %bitcast.k_hbm, bf16[64,2048,256]{2,1,0:T(8,128)(2,1)} %bitcast.1.v_hbm, bf16[1,3072]{1,0:T(2,128)(2,1)} %reshape.14.ga_hbm, bf16[3072,256]{1,0:T(8,128)(2,1)} %wq_hbm.1, bf16[256,3072]{1,0:T(8,128)(2,1)} %wo_hbm.1, ...), custom_call_target="tpu_custom_call" | custom-call | tf_op jit(solution)/shard_map/pallas_call | solution.py:289
  91.3 1.8 %copy.13 = bf16[64,3072]{1,0:T(8,128)(2,1)} copy(bf16[64,3072]{1,0:T(8,128)(2,1)} %shard_map.109) | data formatting | bytes 786432

commit v2 on v1

--- a/solution.py
+++ b/solution.py
@@ -10,7 +10,7 @@
 
 THETA = 10000
 EPS = 1e-6
-GROUP = 8
+GROUP = 16
 PIECE = 4
 CHUNK = 16
 SUB = 8
@@ -28,7 +28,7 @@
 
 
 def kernel(n, x_hbm, k_hbm, v_hbm, ga_hbm, wq_hbm, wo_hbm, gm_hbm, wg_hbm, wu_hbm, wd_hbm, trig_hbm, out_ref,
-           x_v, ga_v, gm_v, trig_v, wq_v, wo_v, wg_v, wu_v, wd_v, ring, x32, h32, q32, seen32, act, hidden,
+           x_v, ga_v, gm_v, trig_v, wq_v, wo_v, wg_v, wu_v, wd_v, ring, x32, h32, q32, seen32, scores, act, hidden,
            own1, term1, rs1, hb, own2, term2, rs2, yb,
            in_sem, w_sem, ring_sem, send1, recv1, send2, recv2, send3, recv3, send4, recv4):
     me = lax.axis_index("tp")
@@ -55,14 +55,13 @@
     ]
     weights = [fetch(wg_hbm, wg_v, w_sem.at[0]), fetch(wu_hbm, wu_v, w_sem.at[1]), fetch(wd_hbm, wd_v, w_sem.at[2])]
 
-    def piece(g, j):
-        src = k_hbm if j < 2 else v_hbm
-        return fetch(src.at[pl.ds(g * GROUP + (j % 2) * PIECE, PIECE)], ring.at[j], ring_sem.at[j])
+    def piece(src, g, j):
+        return fetch(src.at[pl.ds(g * GROUP + j * PIECE, PIECE)], ring.at[j], ring_sem.at[j])
 
     for c in small[:4]:
         c.start()
-    for j in range(4):
-        piece(0, j).start()
+    for j in range(GROUP // PIECE):
+        piece(k_hbm, 0, j).start()
     for c in small[4:]:
         c.start()
 
@@ -127,49 +126,54 @@
         gather(hb.at[c], send2.at[c], recv2.at[c])
 
     row_of = lax.broadcasted_iota(jnp.int32, (GROUP, 1), 0)
+    pieces = GROUP // PIECE
 
     def group(g, carry):
-        def refill(j):
-            @pl.when(g < groups - 1)
-            def _():
-                piece(g + 1, j).start()
-
-            if j < 3:
-                @pl.when(g == groups - 1)
-                def _():
-                    weights[j].start()
-
-        qg = q32[pl.ds(pl.multiple_of(g * GROUP, GROUP), GROUP), :]
-        s = None
-        for j in range(2):
-            piece(g, j).wait()
+        at = pl.ds(pl.multiple_of(g * GROUP, GROUP), GROUP)
+
+        def scores_of(j, carry):
+            qg = q32[at, :]
+            piece(k_hbm, g, j).wait()
+            s = None
             for i in range(PIECE):
                 qm = jnp.where(row_of == j * PIECE + i, qg, 0.0).astype(BF16)
                 t = lax.dot_general(qm, ring[j, i], (((1,), (1,)), ((), ())), preferred_element_type=F32)
                 s = t if s is None else s + t
-            refill(j)
-        s = s * head**-0.5
+            scores[...] = jnp.where(row_of // PIECE == j, s, scores[...])
+            piece(v_hbm, g, j).start()
+            return carry
+
+        def seen_of(j, carry):
+            piece(v_hbm, g, j).wait()
+            o = []
+            for i in range(PIECE):
+                wm = jnp.where(row_of == j * PIECE + i, scores[...], 0.0).astype(BF16)
+                o.append(dot(wm, ring[j, i]))
+            o = jnp.where(row_of < j * PIECE + PIECE // 2, sum(o[1 : PIECE // 2], o[0]), sum(o[PIECE // 2 + 1 :], o[PIECE // 2]))
+            seen32[at, :] = jnp.where(row_of // PIECE == j, o, seen32[at, :])
+
+            @pl.when(g < groups - 1)
+            def _():
+                piece(k_hbm, g + 1, j).start()
+
+            for w in range(3):
+                @pl.when(jnp.logical_and(g == groups - 1, j == w))
+                def _():
+                    weights[w].start()
+
+            return carry
+
+        lax.fori_loop(0, pieces, scores_of, 0)
+        s = scores[...] * head**-0.5
         p = jnp.exp(s - jnp.max(s, -1, keepdims=True))
-        w = p / jnp.sum(p, -1, keepdims=True)
-        o = None
-        for j in range(2, 4):
-            piece(g, j).wait()
-            for i in range(PIECE):
-                wm = jnp.where(row_of == (j - 2) * PIECE + i, w, 0.0).astype(BF16)
-                t = dot(wm, ring[j, i])
-                o = t if o is None else o + t
-            refill(j)
-        seen32[pl.ds(pl.multiple_of(g * GROUP, GROUP), GROUP), :] = o
-        per = CHUNK // GROUP
-
-        @pl.when(lax.rem(g, per) == per - 1)
+        scores[...] = p / jnp.sum(p, -1, keepdims=True)
+        lax.fori_loop(0, pieces, seen_of, 0)
+
+        @pl.when(g > 0)
         def _():
-            send_first(g // per)
-
-        @pl.when(jnp.logical_and(lax.rem(g, per) == 0, g > 0))
-        def _():
-            sum_first(g // per - 1)
-
+            sum_first(g - 1)
+
+        send_first(g)
         return carry
 
     lax.fori_loop(0, groups, group, 0)
@@ -263,11 +267,12 @@
                 pltpu.VMEM((d, ff), BF16),
                 pltpu.VMEM((d, ff), BF16),
                 pltpu.VMEM((ff, d), BF16),
-                pltpu.VMEM((4, PIECE, cache, head), BF16),
+                pltpu.VMEM((GROUP // PIECE, PIECE, cache, head), BF16),
                 pltpu.VMEM((rows, d), F32),
                 pltpu.VMEM((rows, d), F32),
                 pltpu.VMEM((rows, head), F32),
                 pltpu.VMEM((rows, head), F32),
+                pltpu.VMEM((GROUP, cache), F32),
                 pltpu.VMEM((rows, d), BF16),
                 pltpu.VMEM((rows, ff), BF16),
                 pltpu.VMEM((n, *share), F32),
@@ -280,7 +285,7 @@
                 pltpu.VMEM((chunks, n, *share), BF16),
                 dma((6,)),
                 dma((3,)),
-                dma((4,)),
+                dma((GROUP // PIECE,)),
             ]
             + [dma((chunks,))] * 8,
             compiler_params=pltpu.CompilerParams(collective_id=0, has_side_effects=True, vmem_limit_bytes=63 * 2**20),

time: 93.2 us -> 81 us (0.87)
  Pallas kernels: 88.7 us -> 76.4 us
    pallas_call x1, Pallas kernels: 88.7 us -> 76.4 us  [step(): call(x, k_cache.reshape(flat), v_cache.reshape(flat), gain_a.reshape(1, d...]
where the time goes in v2:
time: 81 us; the launch traced here: 80.8 us
  Pallas kernels  76.4 us (94%)
  local copies, waits for them, and re-layouts  4.36 us (5%)
    pallas_call x1, Pallas kernels, step(): call(x, k_cache.reshape(flat), v_cache.reshape(flat), gain_a.reshape(1, d...  76.4 us
    unnamed x1, local copies, waits for them, and re-layouts  1.77 us

profile of v2, /device:TPU:96, one launch (start us, length us, event | category | flops | bytes accessed | tf_op | source)
XLA Modules:
  0.0 80.8 jit_solution(1731347995182337998)
XLA Ops:
  0.0 1.3 %reshape.14.ga_hbm = bf16[1,3072]{1,0:T(2,128)(2,1)} reshape(bf16[3072]{0:T(1024)(128)(2,1)} %param.14) | data formatting | bytes 12288 | tf_op jit(solution)/shard_map/reshape | solution.py:295
  1.3 1.3 %reshape.15.gm_hbm = bf16[1,3072]{1,0:T(2,128)(2,1)} reshape(bf16[3072]{0:T(1024)(128)(2,1)} %param.17) | data formatting | bytes 12288 | tf_op jit(solution)/shard_map/reshape | solution.py:295
  2.6 76.4 %shard_map.109 = bf16[64,3072]{1,0:T(8,128)(2,1)} custom-call(bf16[64,3072]{1,0:T(8,128)(2,1)} %x_hbm.1, bf16[64,2048,256]{2,1,0:T(8,128)(2,1)} %bitcast.k_hbm, bf16[64,2048,256]{2,1,0:T(8,128)(2,1)} %bitcast.1.v_hbm, bf16[1,3072]{1,0:T(2,128)(2,1)} %reshape.14.ga_hbm, bf16[3072,256]{1,0:T(8,128)(2,1)} %wq_hbm.1, bf16[256,3072]{1,0:T(8,128)(2,1)} %wo_hbm.1, ...), custom_call_target="tpu_custom_call" | custom-call | tf_op jit(solution)/shard_map/pallas_call | solution.py:294
  79.0 1.8 %copy.13 = bf16[64,3072]{1,0:T(8,128)(2,1)} copy(bf16[64,3072]{1,0:T(8,128)(2,1)} %shard_map.109) | data formatting | bytes 786432

commit v3 on v2

--- a/solution.py
+++ b/solution.py
@@ -29,7 +29,7 @@
 
 def kernel(n, x_hbm, k_hbm, v_hbm, ga_hbm, wq_hbm, wo_hbm, gm_hbm, wg_hbm, wu_hbm, wd_hbm, trig_hbm, out_ref,
            x_v, ga_v, gm_v, trig_v, wq_v, wo_v, wg_v, wu_v, wd_v, ring, x32, h32, q32, seen32, scores, act, hidden,
-           own1, term1, rs1, hb, own2, term2, rs2, yb,
+           gates, own1, term1, rs1, hb, own2, term2, rs2, yb, own3, term3, rs3, yc,
            in_sem, w_sem, ring_sem, send1, recv1, send2, recv2, send3, recv3, send4, recv4):
     me = lax.axis_index("tp")
     rows, d = x_v.shape
@@ -37,10 +37,8 @@
     half = head // 2
     groups = rows // GROUP
     chunks = rows // CHUNK
-    cols1 = d * CHUNK // (n * SUB)
-    per_row1 = d // cols1
-    width2 = d // chunks
-    per_row2 = width2 // cols1
+    across = n * SUB // CHUNK
+    wide1 = d // across
 
     def fetch(src, dst, sem):
         return pltpu.make_async_copy(src, dst, sem)
@@ -73,7 +71,7 @@
     small[1].wait()
     wide = x_v[...].astype(F32)
     x32[...] = wide
-    act[...] = normed(wide, ga_v[...].astype(F32))
+    act[...] = normed(wide, ga_v[...].astype(F32).reshape(1, d))
     small[2].wait()
     small[3].wait()
     q = dot(act[...], wq_v[...]).astype(BF16).astype(F32)
@@ -88,42 +86,52 @@
     def total(buf, sem):
         fetch(buf.at[pl.ds(0, n - 1)], buf.at[pl.ds(0, n - 1)], sem).wait()
 
-    def scatter(term, land, send, recv):
-        for r in range(1, n):
-            to = lax.rem(me + r, n)
-            pltpu.make_async_remote_copy(
-                src_ref=term.at[to], dst_ref=land.at[r - 1], send_sem=send, recv_sem=recv, device_id={"tp": to}, device_id_type=MESH
-            ).start()
+    def send_to(to, src, dst, send, recv):
+        pltpu.make_async_remote_copy(
+            src_ref=src, dst_ref=dst, send_sem=send, recv_sem=recv, device_id={"tp": to}, device_id_type=MESH
+        ).start()
 
     def gather(buf, send, recv):
         for r in range(1, n):
-            to = lax.rem(me + r, n)
-            pltpu.make_async_remote_copy(
-                src_ref=buf.at[me], dst_ref=buf.at[me], send_sem=send, recv_sem=recv, device_id={"tp": to}, device_id_type=MESH
-            ).start()
-
-    def summed(own, land):
+            send_to(lax.rem(me + r, n), buf.at[me], buf.at[me], send, recv)
+
+    def share_of(states, row, buf):
+        tall, wide = buf.shape[1:]
+        row = pl.multiple_of(row + me // across * tall, SUB)
+        return states[pl.ds(row, tall), pl.ds(pl.multiple_of(lax.rem(me, across) * wide, 128), wide)]
+
+    def finish(states, row, own, land, buf, recv, send_next, recv_next):
+        total(land, recv)
         s = own[me]
         for r in range(n - 1):
             s = s + land[r].astype(F32)
-        return s
+        buf[me] = (share_of(states, row, buf) + s).astype(BF16)
+        gather(buf, send_next, recv_next)
+
+    def whole(buf):
+        rows_of = [jnp.concatenate([buf[rg * across + cg].astype(F32) for cg in range(across)], 1) for rg in range(n // across)]
+        return jnp.concatenate(rows_of, 0)
 
     def send_first(c):
         res = dot(seen32[pl.ds(pl.multiple_of(c * CHUNK, CHUNK), CHUNK), :].astype(BF16), wo_v[...])
-        for s in range(n):
-            rg, cg = divmod(s, per_row1)
-            part = res[rg * SUB : (rg + 1) * SUB, cg * cols1 : (cg + 1) * cols1]
-            own1[s] = part
-            term1[c, s] = part.astype(BF16)
-        scatter(term1.at[c], rs1.at[c], send1.at[c], recv1.at[c])
+        for to in range(n):
+            rg, cg = divmod(to, across)
+            part = res[rg * SUB : (rg + 1) * SUB, cg * wide1 : (cg + 1) * wide1]
+            own1[c, to] = part
+            term1[c, to] = part.astype(BF16)
+        for r in range(1, n):
+            to = lax.rem(me + r, n)
+            send_to(to, term1.at[c, to], rs1.at[c, r - 1], send1.at[c], recv1.at[c])
 
     def sum_first(c):
-        total(rs1.at[c], recv1.at[c])
-        s = summed(own1, rs1.at[c])
-        row = pl.multiple_of(c * CHUNK + me // per_row1 * SUB, SUB)
-        col = pl.multiple_of(lax.rem(me, per_row1) * cols1, 128)
-        hb[c, me] = (x32[pl.ds(row, SUB), pl.ds(col, cols1)] + s).astype(BF16)
-        gather(hb.at[c], send2.at[c], recv2.at[c])
+        finish(x32, c * CHUNK, own1.at[c], rs1.at[c], hb.at[c], recv1.at[c], send2.at[c], recv2.at[c])
+
+    def norm_first(c):
+        total(hb.at[c], recv2.at[c])
+        h = whole(hb.at[c])
+        at = pl.ds(pl.multiple_of(c * CHUNK, CHUNK), CHUNK)
+        h32[at, :] = h
+        act[at, :] = normed(h, gm_v[...].astype(F32).reshape(1, d))
 
     row_of = lax.broadcasted_iota(jnp.int32, (GROUP, 1), 0)
     pieces = GROUP // PIECE
@@ -167,74 +175,99 @@
         s = scores[...] * head**-0.5
         p = jnp.exp(s - jnp.max(s, -1, keepdims=True))
         scores[...] = p / jnp.sum(p, -1, keepdims=True)
-        lax.fori_loop(0, pieces, seen_of, 0)
 
         @pl.when(g > 0)
         def _():
             sum_first(g - 1)
 
+        @pl.when(g > 1)
+        def _():
+            norm_first(g - 2)
+
+        lax.fori_loop(0, pieces, seen_of, 0)
         send_first(g)
         return carry
 
     lax.fori_loop(0, groups, group, 0)
+    passes = [
+        (0, rows - CHUNK, own2, term2, rs2, yb, 0),
+        (rows - CHUNK, CHUNK, own3, term3, rs3, yc, 1),
+    ]
+    ff = wg_v.shape[1]
+    block = ff // 2
+
+    def gate(p):
+        lo, tall = passes[p][:2]
+
+        def body(i, carry):
+            at = pl.ds(pl.multiple_of(i * block, block), block)
+            gates[lo : lo + tall, at] = dot(act[lo : lo + tall, :], wg_v[:, at])
+            return carry
+
+        lax.fori_loop(0, ff // block, body, 0)
+
+    def up(p):
+        lo, tall = passes[p][:2]
+
+        def body(i, carry):
+            at = pl.ds(pl.multiple_of(i * block, block), block)
+            u = dot(act[lo : lo + tall, :], wu_v[:, at])
+            hidden[lo : lo + tall, at] = (jax.nn.silu(gates[lo : lo + tall, at]) * u).astype(BF16)
+            return carry
+
+        lax.fori_loop(0, ff // block, body, 0)
+
+    def both(p):
+        lo, tall = passes[p][:2]
+        for i in range(0, ff, block):
+            g = dot(act[lo : lo + tall, :], wg_v[:, i : i + block])
+            u = dot(act[lo : lo + tall, :], wu_v[:, i : i + block])
+            hidden[lo : lo + tall, i : i + block] = (jax.nn.silu(g) * u).astype(BF16)
+
+    def down(p):
+        lo, tall, own, term, land, _, k = passes[p]
+        tall1 = tall // (n // across)
+
+        def body(i, carry):
+            at = lax.rem(me + i, across // 2)
+            res = dot(hidden[lo : lo + tall, :], wd_v[:, pl.ds(pl.multiple_of(at * 2 * wide1, 2 * wide1), 2 * wide1)])
+            for cg in range(2):
+                for rg in range(n // across):
+                    to = rg * across + at * 2 + cg
+                    part = res[rg * tall1 : (rg + 1) * tall1, cg * wide1 : (cg + 1) * wide1]
+                    own[to] = part
+                    term[to] = part.astype(BF16)
+
+                    @pl.when(to != me)
+                    def _():
+                        send_to(to, term.at[to], land.at[lax.rem(to - me + n, n) - 1], send3.at[k], recv3.at[k])
+
+            return carry
+
+        lax.fori_loop(0, across // 2, body, 0)
+
+    norm_first(chunks - 2)
+    weights[0].wait()
+    gate(0)
     sum_first(chunks - 1)
-
-    gm = gm_v[...].astype(F32)
-    for c in range(chunks):
-        total(hb.at[c], recv2.at[c])
-        h = jnp.concatenate(
-            [
-                jnp.concatenate([hb[c, rg * per_row1 + cg].astype(F32) for cg in range(per_row1)], 1)
-                for rg in range(CHUNK // SUB)
-            ],
-            0,
-        )
-        h32[c * CHUNK : (c + 1) * CHUNK, :] = h
-        act[c * CHUNK : (c + 1) * CHUNK, :] = normed(h, gm)
-
-    weights[0].wait()
     weights[1].wait()
-    block = 256
-
-    def up(i, carry):
-        at = pl.ds(pl.multiple_of(i * block, block), block)
-        gate = dot(act[...], wg_v[:, at])
-        hidden[:, at] = (jax.nn.silu(gate) * dot(act[...], wu_v[:, at])).astype(BF16)
-        return carry
-
-    lax.fori_loop(0, wg_v.shape[1] // block, up, 0)
+    up(0)
     weights[2].wait()
-
-    for c in range(chunks):
-        res = dot(hidden[...], wd_v[:, c * width2 : (c + 1) * width2])
-        for s in range(n):
-            rg, cg = divmod(s, per_row2)
-            part = res[rg * SUB : (rg + 1) * SUB, cg * cols1 : (cg + 1) * cols1]
-            own2[c, s] = part
-            term2[c, s] = part.astype(BF16)
-        scatter(term2.at[c], rs2.at[c], send3.at[c], recv3.at[c])
-
-    for c in range(chunks):
-        total(rs2.at[c], recv3.at[c])
-        s = summed(own2.at[c], rs2.at[c])
-        row = pl.multiple_of(me // per_row2 * SUB, SUB)
-        col = pl.multiple_of(c * width2 + lax.rem(me, per_row2) * cols1, 128)
-        yb[c, me] = (h32[pl.ds(row, SUB), pl.ds(col, cols1)] + s).astype(BF16)
-        gather(yb.at[c], send4.at[c], recv4.at[c])
-
-    for c in range(chunks):
-        total(yb.at[c], recv4.at[c])
-        for rg in range(0, rows // SUB, 2):
-            for cg in range(per_row2):
-                pair = [yb[c, (rg + k) * per_row2 + cg].astype(F32) for k in range(2)]
-                col = c * width2 + cg * cols1
-                out_ref[rg * SUB : (rg + 2) * SUB, col : col + cols1] = jnp.concatenate(pair, 0).astype(BF16)
-
+    down(0)
+    norm_first(chunks - 1)
+    both(1)
+    down(1)
+    for lo, tall, own, term, land, buf, k in passes:
+        finish(h32, lo, own, land, buf, recv3.at[k], send4.at[k], recv4.at[k])
+    for lo, tall, own, term, land, buf, k in passes:
+        total(buf, recv4.at[k])
+        out_ref[lo : lo + tall, :] = whole(buf).astype(BF16)
     for c in range(chunks):
         total(term1.at[c], send1.at[c])
         total(hb.at[c], send2.at[c])
-        total(term2.at[c], send3.at[c])
-        total(yb.at[c], send4.at[c])
+    for lo, tall, own, term, land, buf, k in passes:
+        total(term, send3.at[k])
+        total(buf, send4.at[k])
 
 
 def solution(mesh):
@@ -259,8 +292,8 @@
             out_specs=pl.BlockSpec(memory_space=pltpu.VMEM),
             scratch_shapes=[
                 pltpu.VMEM((rows, d), BF16),
-                pltpu.VMEM((1, d), BF16),
-                pltpu.VMEM((1, d), BF16),
+                pltpu.VMEM((d,), BF16),
+                pltpu.VMEM((d,), BF16),
                 pltpu.VMEM((2, half), F32),
                 pltpu.VMEM((d, head), BF16),
                 pltpu.VMEM((head, d), BF16),
@@ -275,24 +308,29 @@
                 pltpu.VMEM((GROUP, cache), F32),
                 pltpu.VMEM((rows, d), BF16),
                 pltpu.VMEM((rows, ff), BF16),
-                pltpu.VMEM((n, *share), F32),
-                pltpu.VMEM((chunks, n, *share), BF16),
-                pltpu.VMEM((chunks, n - 1, *share), BF16),
-                pltpu.VMEM((chunks, n, *share), BF16),
+                pltpu.VMEM((rows, ff), F32),
                 pltpu.VMEM((chunks, n, *share), F32),
                 pltpu.VMEM((chunks, n, *share), BF16),
                 pltpu.VMEM((chunks, n - 1, *share), BF16),
                 pltpu.VMEM((chunks, n, *share), BF16),
+            ]
+            + [
+                pltpu.VMEM((m, t, share[1]), kind)
+                for t in (SUB * (chunks - 1), SUB)
+                for m, kind in ((n, F32), (n, BF16), (n - 1, BF16), (n, BF16))
+            ]
+            + [
                 dma((6,)),
                 dma((3,)),
                 dma((GROUP // PIECE,)),
             ]
-            + [dma((chunks,))] * 8,
+            + [dma((chunks,))] * 4
+            + [dma((2,))] * 4,
             compiler_params=pltpu.CompilerParams(collective_id=0, has_side_effects=True, vmem_limit_bytes=63 * 2**20),
         )
         flat = (rows, cache, head)
         return call(
-            x, k_cache.reshape(flat), v_cache.reshape(flat), gain_a.reshape(1, d), wq, wo, gain_m.reshape(1, d), w_gate, w_up, w_down, trig
+            x, k_cache.reshape(flat), v_cache.reshape(flat), gain_a, wq, wo, gain_m, w_gate, w_up, w_down, trig
         )
 
     states, cache, columns, rows_of = P("dp", None), P("dp", None, "tp", None), P(None, "tp"), P("tp", None)

time: 81 us -> 73.6 us (0.909)
  Pallas kernels: 76.4 us -> 71.7 us
  local copies, waits for them, and re-layouts: 4.36 us -> 1.77 us
    pallas_call x1, Pallas kernels: 76.4 us -> 71.7 us  [step(): call(x, k_cache.reshape(flat), v_cache.reshape(flat), gain_a, wq, wo, gai...]
    reshape x2 -> x0, local copies, waits for them, and re-layouts: 2.59 us -> none  [the longest x1 1.3 us: step(): gain_a.reshape(1, d)]
where the time goes in v3:
time: 73.6 us; the launch traced here: 73.5 us
  Pallas kernels  71.7 us (97%)
  local copies, waits for them, and re-layouts  1.77 us (2%)
    pallas_call x1, Pallas kernels, step(): call(x, k_cache.reshape(flat), v_cache.reshape(flat), gain_a, wq, wo, gai...  71.7 us
    unnamed x1, local copies, waits for them, and re-layouts  1.77 us

profile of v3, /device:TPU:96, one launch (start us, length us, event | category | flops | bytes accessed | tf_op | source)
XLA Modules:
  0.0 73.5 jit_solution(7813414780167563881)
XLA Ops:
  0.0 71.7 %shard_map.109 = bf16[64,3072]{1,0:T(8,128)(2,1)} custom-call(bf16[64,3072]{1,0:T(8,128)(2,1)} %x_hbm.1, bf16[64,2048,256]{2,1,0:T(8,128)(2,1)} %bitcast.k_hbm, bf16[64,2048,256]{2,1,0:T(8,128)(2,1)} %bitcast.1.v_hbm, bf16[3072]{0:T(1024)(128)(2,1)} %ga_hbm.1, bf16[3072,256]{1,0:T(8,128)(2,1)} %wq_hbm.1, bf16[256,3072]{1,0:T(8,128)(2,1)} %wo_hbm.1, ...), custom_call_target="tpu_custom_call" | custom-call | tf_op jit(solution)/shard_map/pallas_call | solution.py:332
  71.7 1.8 %copy.13 = bf16[64,3072]{1,0:T(8,128)(2,1)} copy(bf16[64,3072]{1,0:T(8,128)(2,1)} %shard_map.109) | data formatting | bytes 786432

commit v4 on v3

--- a/solution.py
+++ b/solution.py
@@ -283,11 +283,11 @@
         trig = jnp.asarray(np.stack([np.cos(angle), np.sin(angle)]).astype(np.float32))
         chunks = rows // CHUNK
         share = (SUB, rows * d // chunks // n // SUB)
-        any_spec = pl.BlockSpec(memory_space=pl.ANY)
+        any_spec = pl.BlockSpec(memory_space=pltpu.HBM)
         dma = pltpu.SemaphoreType.DMA
         call = pl.pallas_call(
             functools.partial(kernel, n),
-            out_shape=jax.ShapeDtypeStruct((rows, d), BF16),
+            out_shape=pltpu.VMEM((rows, d), BF16),
             in_specs=[any_spec] * 11,
             out_specs=pl.BlockSpec(memory_space=pltpu.VMEM),
             scratch_shapes=[
@@ -326,7 +326,7 @@
             ]
             + [dma((chunks,))] * 4
             + [dma((2,))] * 4,
-            compiler_params=pltpu.CompilerParams(collective_id=0, has_side_effects=True, vmem_limit_bytes=63 * 2**20),
+            compiler_params=pltpu.CompilerParams(collective_id=0, has_side_effects=True, vmem_limit_bytes=58 * 2**20),
         )
         flat = (rows, cache, head)
         return call(

time: 73.6 us -> 71.9 us (0.977)
  local copies, waits for them, and re-layouts: 1.77 us -> 0.75 us
    unnamed x1, local copies, waits for them, and re-layouts: 1.77 us -> 0.75 us
    pallas_call x1, Pallas kernels: 71.7 us -> 71 us  [step(): call(x, k_cache.reshape(flat), v_cache.reshape(flat), gain_a, wq, wo, gai...]
where the time goes in v4:
time: 71.9 us; the launch traced here: 71.8 us
  Pallas kernels  71 us (99%)
  local copies, waits for them, and re-layouts  0.75 us (1%)
    pallas_call x1, Pallas kernels, step(): call(x, k_cache.reshape(flat), v_cache.reshape(flat), gain_a, wq, wo, gai...  71 us

profile of v4, /device:TPU:96, one launch (start us, length us, event | category | flops | bytes accessed | tf_op | source)
XLA Modules:
  0.0 71.8 jit_solution(9272961867104119300)
XLA Ops:
  0.0 71.0 %shard_map.109 = bf16[64,3072]{1,0:T(8,128)(2,1)S(1)} custom-call(bf16[64,3072]{1,0:T(8,128)(2,1)} %x_hbm.1, bf16[64,2048,256]{2,1,0:T(8,128)(2,1)} %bitcast.k_hbm, bf16[64,2048,256]{2,1,0:T(8,128)(2,1)} %bitcast.1.v_hbm, bf16[3072]{0:T(1024)(128)(2,1)} %ga_hbm.1, bf16[3072,256]{1,0:T(8,128)(2,1)} %wq_hbm.1, bf16[256,3072]{1,0:T(8,128)(2,1)} %wo_hbm.1, ...), custom_call_target="tpu_custom_call" | custom-call | tf_op jit(solution)/shard_map/pallas_call | solution.py:332
  71.0 0.7 %copy.13 = bf16[64,3072]{1,0:T(8,128)(2,1)} copy(bf16[64,3072]{1,0:T(8,128)(2,1)S(1)} %shard_map.109) | data formatting | bytes 786432
